TPU v7x, 128 devices: a whole 4x4x4 slice. The times are simulated.
128 devices in a mesh: lat: 16 (over z, y_lo, core), lon: 8 (over y_hi, x).
Axes of the slice: x: 4, y: 4 (y_hi: 2, y_lo: 2; y = y_hi * 2 + y_lo), z: 4, core: 2. Of those that a mesh axis runs over, the one named last changes fastest.
Arguments:
- field: bfloat16 [256, 256, 256], P('lat', 'lon'), may hold values from -6 to 6
- weights: bfloat16 [16, 8, 3072, 3072], P('lat', 'lon'), may hold values from -0.09375 to 0.09375
- strip_ids: int32 [16, 8], P('lat'), may hold values from 0 to 63, as said below
- counts: int32 [16], P('lat'), may hold values from 2 to 8, as said below
Outputs:
- remapped: bfloat16 [131072, 256], P(('lat', 'lon'))
Inputs may be any that keep to these rules, and one draw needn't show every extreme that they name: `strip_ids`: row b holds consecutive global strip numbers, the last one repeated where the run meets the end of its window, all among the strips of source bands b - 2 to b + 2, band c holding strips 4 * c to 4 * c + 3. Band b uses the first counts[b] slots of its row.
All inputs are finite; a program needn't handle non-finite values.
Results may differ from a plain program's by a relative error of at most 0.0059.
Values may be sent and summed in bfloat16 or wider, within the bound.
A program may use at most 64 MiB of HBM per device.

v0:
```python
import jax
import jax.numpy as jnp
from jax import lax
from jax.sharding import PartitionSpec as P

STRIP_ROWS = 4
SLOTS = 8
REACH = 2


def extended(cells, sides, width, closed):
    for axis, dim in sides:
        count = lax.axis_size(axis)
        ends = count if closed else count - 1
        head = lax.slice_in_dim(cells, 0, width, axis=dim)
        tail = lax.slice_in_dim(cells, cells.shape[dim] - width, cells.shape[dim], axis=dim)
        cells = jnp.concatenate(
            [
                lax.ppermute(tail, axis, [(i, (i + 1) % count) for i in range(ends)]),
                cells,
                lax.ppermute(head, axis, [((i + 1) % count, i) for i in range(ends)]),
            ],
            axis=dim,
        )
    return cells


def from_behind(block, axis, distance):
    devices = range(lax.axis_size(axis))
    route = [(i - distance, i) for i in devices if i - distance in devices]
    return lax.ppermute(block, axis, route)


def passed_along(block, axis, distance):
    devices = range(lax.axis_size(axis))
    route = [((i - distance) % len(devices), i) for i in devices]
    return lax.ppermute(block, axis, route)


def strip_stack(padded, strip_rows):
    values = padded.astype(jnp.float32)
    centre = padded[1:-1, 1:-1]
    eastward = ((values[1:-1, 2:] - values[1:-1, :-2]) * 0.5).astype(jnp.bfloat16)
    northward = ((values[2:, 1:-1] - values[:-2, 1:-1]) * 0.5).astype(jnp.bfloat16)
    row_count, lon_count, chan_count = centre.shape
    components = [
        component.reshape(row_count // strip_rows, strip_rows, lon_count, chan_count)
        for component in (centre, eastward, northward)
    ]
    stacked = jnp.stack(components, axis=1)
    return stacked.reshape(row_count // strip_rows, 3 * strip_rows * lon_count, chan_count)


def body(field, weights, strip_ids, counts):
    lon_padded = extended(field, (("lon", 1),), 1, True)
    both_padded = extended(lon_padded, (("lat", 0),), 1, False)
    band_index = lax.axis_index("lat")
    band_count = lax.axis_size("lat")
    upper_ghost = jnp.where(band_index == 0, lon_padded[:1], both_padded[:1])
    lower_ghost = jnp.where(band_index == band_count - 1, lon_padded[-1:], both_padded[-1:])
    padded = jnp.concatenate([upper_ghost, both_padded[1:-1], lower_ghost], axis=0)
    own_strips = strip_stack(padded, STRIP_ROWS)
    per_device = own_strips.shape[0]
    gathered = []
    for reach_step in range(-REACH, REACH + 1):
        if reach_step == 0:
            gathered.append(own_strips)
        else:
            remote_tile = from_behind(padded, "lat", -reach_step)
            gathered.append(strip_stack(remote_tile, STRIP_ROWS))
    neighbourhood = jnp.concatenate(gathered, axis=0)
    local_ids = strip_ids[0] - (band_index - REACH) * per_device
    live_slots = jnp.arange(SLOTS, dtype=jnp.int32) < counts[0]
    picked = jnp.take(neighbourhood, local_ids, axis=0)
    picked = jnp.where(live_slots[:, None, None], picked, jnp.zeros_like(picked))
    slot_width = picked.shape[1]
    chan_count = picked.shape[2]
    picked = picked.reshape(SLOTS * slot_width, chan_count)
    partial_sums = jnp.dot(weights[0, 0], picked, preferred_element_type=jnp.float32)
    sector_rows = partial_sums.shape[0] // 3
    from_west = passed_along(partial_sums[2 * sector_rows :].astype(jnp.bfloat16), "lon", 1).astype(
        jnp.float32
    )
    from_east = passed_along(partial_sums[:sector_rows].astype(jnp.bfloat16), "lon", -1).astype(
        jnp.float32
    )
    total = partial_sums[sector_rows : 2 * sector_rows] + from_west + from_east
    return total.astype(jnp.bfloat16)


def solution(mesh):
    placed = (P("lat", "lon", None), P("lat", "lon", None, None), P("lat", None), P("lat"))
    return jax.shard_map(
        body, mesh=mesh, in_specs=placed, out_specs=P(("lat", "lon"), None), check_vma=False
    )
```

profile of v0, /device:TPU:38, one launch (start us, length us, event | category | flops | bytes accessed | tf_op | source)
XLA Modules:
  0.0 86.4 jit_solution(2380271061009193182)
XLA Ops:
  0.0 0.9 %fusion.30 = (bf16[16,1,256]{2,1,0:T(2,128)(2,1)S(1)}, bf16[16,1,256]{2,1,0:T(2,128)(2,1)S(1)}) fusion(bf16[16,32,256]{2,1,0:T(8,128)(2,1)} %param.4), kind=kLoop, calls=%fused_computation.62 | loop fusion | bytes 32768 | tf_op jit(solution)/shard_map/slice | solution.py:16
  0.9 3.2 %collective-permute-start = (bf16[16,1,256]{2,1,0:T(2,128)(2,1)S(1)}, bf16[16,1,256]{2,1,0:T(2,128)(2,1)S(1)}, u32[]{:S(2)}, u32[]{:S(2)}) collective-permute-start(bf16[16,1,256]{2,1,0:T(2,128)(2,1)S(1)} %get-tuple-element.21), channel_id=1, source_target_pairs={{0,1},{1,2},{2,3},{3,4},{4,5},{5,6},{6,7},{7,0},{8,9},{9,10},{10,1... | collective-permute-start | bytes 24584 | tf_op jit(solution)/shard_map/ppermute | solution.py:19
  4.8 0.7 compare_and_fusion
  5.6 5.9 %collective-permute-done.1 = bf16[16,1,256]{2,1,0:T(2,128)(2,1)S(1)} collective-permute-done((bf16[16,1,256]{2,1,0:T(2,128)(2,1)S(1)}, bf16[16,1,256]{2,1,0:T(2,128)(2,1)S(1)}, u32[]{:S(2)}, u32[]{:S(2)}) %collective-permute-start.1) | collective-permute-done | bytes 8224 | tf_op jit(solution)/shard_map/ppermute | solution.py:21
  11.5 0.7 pad_maximum_fusion.6
  12.2 1.9 %collective-permute-start.2 = (bf16[1,34,256]{2,1,0:T(8,128)(2,1)S(1)}, bf16[1,34,256]{2,1,0:T(8,128)(2,1)S(1)}, u32[]{:S(2)}, u32[]{:S(2)}) collective-permute-start(bf16[1,34,256]{2,1,0:T(8,128)(2,1)S(1)} %pad_maximum_fusion.6), channel_id=1, source_target_pairs={{0,8},{8,16},{16,24},{24,32},{32,40},{40,48},{48,56},{56,64},{64,7... | collective-permute-start | bytes 52232 | tf_op jit(solution)/shard_map/ppermute | solution.py:19
  14.1 0.7 fusion.27
  14.8 3.4 %collective-permute-done.2 = bf16[1,34,256]{2,1,0:T(8,128)(2,1)S(1)} collective-permute-done((bf16[1,34,256]{2,1,0:T(8,128)(2,1)S(1)}, bf16[1,34,256]{2,1,0:T(8,128)(2,1)S(1)}, u32[]{:S(2)}, u32[]{:S(2)}) %collective-permute-start.2) | collective-permute-done | bytes 17440 | tf_op jit(solution)/shard_map/ppermute | solution.py:19
  18.2 0.7 broadcast_select_fusion.1
  18.9 1.9 %collective-permute-start.3 = (bf16[1,34,256]{2,1,0:T(8,128)(2,1)S(1)}, bf16[1,34,256]{2,1,0:T(8,128)(2,1)S(1)}, u32[]{:S(2)}, u32[]{:S(2)}) collective-permute-start(bf16[1,34,256]{2,1,0:T(8,128)(2,1)S(1)} %get-tuple-element.6), channel_id=1, source_target_pairs={{8,0},{16,8},{24,16},{32,24},{40,32},{48,40},{56,48},{64,56},{72,6... | collective-permute-start | bytes 52232 | tf_op jit(solution)/shard_map/ppermute | solution.py:21
  20.9 1.4 %collective-permute-done.3 = bf16[1,34,256]{2,1,0:T(8,128)(2,1)S(1)} collective-permute-done((bf16[1,34,256]{2,1,0:T(8,128)(2,1)S(1)}, bf16[1,34,256]{2,1,0:T(8,128)(2,1)S(1)}, u32[]{:S(2)}, u32[]{:S(2)}) %collective-permute-start.3) | collective-permute-done | bytes 17440 | tf_op jit(solution)/shard_map/ppermute | solution.py:21
  22.3 1.1 %fusion.28 = (f32[18,34,256]{2,1,0:T(8,128)S(1)}, bf16[18,34,256]{2,1,0:T(8,128)(2,1)S(1)}) fusion(bf16[1,34,256]{2,1,0:T(8,128)(2,1)S(1)} %broadcast_select_fusion, bf16[16,1,256]{2,1,0:T(2,128)(2,1)S(1)} %collective-permute-done.1, bf16[16,32,256]{2,1,0:T(8,128)(2,1)} %param.4, bf16[16,1,256]{2,1,0:T(2,128)(2,1)S(1)} %collective-permute-done, ...), kind=kLoop, calls=%fused_computation.60 | loop fusion | flops 1723392 | bytes 1253376 | tf_op jit(solution)/shard_map/convert_element_type | solution.py:41
  23.4 1.9 %collective-permute-start.5 = (bf16[18,34,256]{2,1,0:T(8,128)(2,1)S(1)}, bf16[18,34,256]{2,1,0:T(8,128)(2,1)S(1)}, u32[]{:S(2)}, u32[]{:S(2)}) collective-permute-start(bf16[18,34,256]{2,1,0:T(8,128)(2,1)S(1)} %get-tuple-element.20), channel_id=1, source_target_pairs={{0,8},{8,16},{16,24},{24,32},{32,40},{40,48},{48,56},{56,64},{64,7... | collective-permute-start | bytes 940040 | tf_op jit(solution)/shard_map/ppermute | solution.py:31
  25.4 5.4 %collective-permute-start.4 = (bf16[18,34,256]{2,1,0:T(8,128)(2,1)S(1)}, bf16[18,34,256]{2,1,0:T(8,128)(2,1)S(1)}, u32[]{:S(2)}, u32[]{:S(2)}) collective-permute-start(bf16[18,34,256]{2,1,0:T(8,128)(2,1)S(1)} %get-tuple-element.20), channel_id=1, source_target_pairs={{0,16},{8,24},{16,32},{24,40},{32,48},{40,56},{48,64},{56,72},{64,... | collective-permute-start | bytes 940040 | tf_op jit(solution)/shard_map/ppermute | solution.py:31
  30.7 1.9 %collective-permute-start.6 = (bf16[18,34,256]{2,1,0:T(8,128)(2,1)S(1)}, bf16[18,34,256]{2,1,0:T(8,128)(2,1)S(1)}, u32[]{:S(2)}, u32[]{:S(2)}) collective-permute-start(bf16[18,34,256]{2,1,0:T(8,128)(2,1)S(1)} %get-tuple-element.20), channel_id=1, source_target_pairs={{8,0},{16,8},{24,16},{32,24},{40,32},{48,40},{56,48},{64,56},{72,6... | collective-permute-start | bytes 940040 | tf_op jit(solution)/shard_map/ppermute | solution.py:31
  32.7 2.8 %collective-permute-start.7 = (bf16[18,34,256]{2,1,0:T(8,128)(2,1)S(1)}, bf16[18,34,256]{2,1,0:T(8,128)(2,1)S(1)}, u32[]{:S(2)}, u32[]{:S(2)}) collective-permute-start(bf16[18,34,256]{2,1,0:T(8,128)(2,1)S(1)} %get-tuple-element.20), channel_id=1, source_target_pairs={{16,0},{24,8},{32,16},{40,24},{48,32},{56,40},{64,48},{72,56},{80,... | collective-permute-start | bytes 940040 | tf_op jit(solution)/shard_map/ppermute | solution.py:31
  36.0 3.7 %collective-permute-done.4 = bf16[18,34,256]{2,1,0:T(8,128)(2,1)S(1)} collective-permute-done((bf16[18,34,256]{2,1,0:T(8,128)(2,1)S(1)}, bf16[18,34,256]{2,1,0:T(8,128)(2,1)S(1)}, u32[]{:S(2)}, u32[]{:S(2)}) %collective-permute-start.4) | collective-permute-done | bytes 313376 | tf_op jit(solution)/shard_map/ppermute | solution.py:31
  40.1 0.9 %constant_dynamic-update-slice_fusion.4 = bf16[20,384,256]{2,1,0:T(8,128)(2,1)} fusion(bf16[4,384,256]{2,1,0:T(8,128)(2,1)S(1)} %bitcast.44), kind=kLoop, calls=%fused_computation.53 | loop fusion | bytes 1572864
  41.0 5.6 %collective-permute-done.6 = bf16[18,34,256]{2,1,0:T(8,128)(2,1)S(1)} collective-permute-done((bf16[18,34,256]{2,1,0:T(8,128)(2,1)S(1)}, bf16[18,34,256]{2,1,0:T(8,128)(2,1)S(1)}, u32[]{:S(2)}, u32[]{:S(2)}) %collective-permute-start.6) | collective-permute-done | bytes 313376 | tf_op jit(solution)/shard_map/ppermute | solution.py:31
  46.9 6.5 %collective-permute-done.7 = bf16[18,34,256]{2,1,0:T(8,128)(2,1)S(1)} collective-permute-done((bf16[18,34,256]{2,1,0:T(8,128)(2,1)S(1)}, bf16[18,34,256]{2,1,0:T(8,128)(2,1)S(1)}, u32[]{:S(2)}, u32[]{:S(2)}) %collective-permute-start.7) | collective-permute-done | bytes 313376 | tf_op jit(solution)/shard_map/ppermute | solution.py:31
  53.8 1.0 %constant_dynamic-update-slice_fusion.3 = bf16[20,384,256]{2,1,0:T(8,128)(2,1)} fusion(bf16[20,384,256]{2,1,0:T(8,128)(2,1)} %constant_dynamic-update-slice_fusion.4, bf16[4,384,256]{2,1,0:T(8,128)(2,1)S(1)} %bitcast.41), kind=kLoop, calls=%fused_computation.52 | loop fusion | bytes 1572864
  54.7 0.9 %constant_dynamic-update-slice_fusion.2 = bf16[20,384,256]{2,1,0:T(8,128)(2,1)} fusion(bf16[20,384,256]{2,1,0:T(8,128)(2,1)} %constant_dynamic-update-slice_fusion.3, bf16[4,384,256]{2,1,0:T(8,128)(2,1)S(1)} %bitcast.40), kind=kLoop, calls=%fused_computation.51 | loop fusion | bytes 1572864
  55.8 0.9 %constant_dynamic-update-slice_fusion.1 = bf16[20,384,256]{2,1,0:T(8,128)(2,1)} fusion(bf16[20,384,256]{2,1,0:T(8,128)(2,1)} %constant_dynamic-update-slice_fusion.2, bf16[4,384,256]{2,1,0:T(8,128)(2,1)S(1)} %bitcast.42), kind=kLoop, calls=%fused_computation.50 | loop fusion | bytes 1572864
  57.0 0.9 %constant_dynamic-update-slice_fusion = bf16[20,384,256]{2,1,0:T(8,128)(2,1)} fusion(bf16[20,384,256]{2,1,0:T(8,128)(2,1)} %constant_dynamic-update-slice_fusion.1, bf16[4,384,256]{2,1,0:T(8,128)(2,1)S(1)} %bitcast.43), kind=kLoop, calls=%fused_computation.49 | loop fusion | bytes 1572864 | tf_op jit(solution)/shard_map/concatenate | solution.py:71
  57.9 2.8 %gather_fusion = bf16[8,384,256]{2,1,0:T(8,128)(2,1)S(1)} fusion(bf16[20,384,256]{2,1,0:T(8,128)(2,1)} %constant_dynamic-update-slice_fusion, s32[1024]{0:T(1024)S(1)} %pad_clamp_fusion), kind=kCustom, calls=%fused_computation | custom fusion | bytes 3145760 | tf_op jit(solution)/shard_map/jit(_take)/gather | solution.py:74
  60.7 0.2 select_select_fusion
  60.9 9.1 %fusion.31 = (bf16[3072,256]{0,1:T(8,128)(2,1)S(1)}, f32[3072,256]{0,1:T(8,128)S(1)}) fusion(bf16[3072,256]{1,0:T(8,128)(2,1)S(1)} %bitcast.45, bf16[1,1,3072,3072]{3,2,1,0:T(8,128)(2,1)} %param.5), kind=kOutput, calls=%fused_computation.63 | convolution fusion | flops 4832624640 | bytes 25165824 | tf_op jit(solution)/shard_map/dot_general | solution.py:79
  70.1 2.0 %collective-permute-start.9 = (bf16[1024,256]{0,1:T(8,128)(2,1)S(1)}, bf16[1024,256]{0,1:T(8,128)(2,1)S(1)}, u32[]{:S(2)}, u32[]{:S(2)}) collective-permute-start(bf16[1024,256]{0,1:T(8,128)(2,1)S(1)} %get-tuple-element.8), channel_id=1, source_target_pairs={{1,0},{2,1},{3,2},{4,3},{5,4},{6,5},{7,6},{0,7},{9,8},{10,9},{11,1... | collective-permute-start | bytes 1572872 | tf_op jit(solution)/shard_map/ppermute | solution.py:37
  72.1 9.3 %collective-permute-done.8 = bf16[1024,256]{0,1:T(8,128)(2,1)S(1)} collective-permute-done((bf16[1024,256]{0,1:T(8,128)(2,1)S(1)}, bf16[1024,256]{0,1:T(8,128)(2,1)S(1)}, u32[]{:S(2)}, u32[]{:S(2)}) %collective-permute-start.8) | collective-permute-done | bytes 524320 | tf_op jit(solution)/shard_map/ppermute | solution.py:37
  81.5 3.7 %collective-permute-done.9 = bf16[1024,256]{0,1:T(8,128)(2,1)S(1)} collective-permute-done((bf16[1024,256]{0,1:T(8,128)(2,1)S(1)}, bf16[1024,256]{0,1:T(8,128)(2,1)S(1)}, u32[]{:S(2)}, u32[]{:S(2)}) %collective-permute-start.9) | collective-permute-done | bytes 524320 | tf_op jit(solution)/shard_map/ppermute | solution.py:37
  85.2 0.2 fusion.6
  85.4 1.0 %copy.6 = bf16[1024,256]{1,0:T(8,128)(2,1)} copy(bf16[1024,256]{0,1:T(8,128)(2,1)S(1)} %fusion.6) | data formatting | bytes 1048576 | tf_op jit(solution)/shard_map/convert_element_type | solution.py:88
  (27 shorter events, 2.1 us)
Async XLA Ops:
  0.0 35.7 %copy-start = (bf16[16,32,256]{2,1,0:T(8,128)(2,1)S(1)}, bf16[16,32,256]{2,1,0:T(8,128)(2,1)}, u32[]{:S(2)}) copy-start(bf16[16,32,256]{2,1,0:T(8,128)(2,1)} %param.4) | copy-start | bytes 786436
  0.9 4.6 %collective-permute-start = (bf16[16,1,256]{2,1,0:T(2,128)(2,1)S(1)}, bf16[16,1,256]{2,1,0:T(2,128)(2,1)S(1)}, u32[]{:S(2)}, u32[]{:S(2)}) collective-permute-start(bf16[16,1,256]{2,1,0:T(2,128)(2,1)S(1)} %get-tuple-element.21), channel_id=1, source_target_pairs={{0,1},{1,2},{2,3},{3,4},{4,5},{5,6},{6,7},{7,0},{8,9},{9,10},{10,1... | collective-permute-start | bytes 24584 | tf_op jit(solution)/shard_map/ppermute | solution.py:19
  4.1 7.4 %collective-permute-start.1 = (bf16[16,1,256]{2,1,0:T(2,128)(2,1)S(1)}, bf16[16,1,256]{2,1,0:T(2,128)(2,1)S(1)}, u32[]{:S(2)}, u32[]{:S(2)}) collective-permute-start(bf16[16,1,256]{2,1,0:T(2,128)(2,1)S(1)} %get-tuple-element.22), channel_id=1, source_target_pairs={{1,0},{2,1},{3,2},{4,3},{5,4},{6,5},{7,6},{0,7},{9,8},{10,9},{11,1... | collective-permute-start | bytes 24584 | tf_op jit(solution)/shard_map/ppermute | solution.py:21
  12.2 6.0 %collective-permute-start.2 = (bf16[1,34,256]{2,1,0:T(8,128)(2,1)S(1)}, bf16[1,34,256]{2,1,0:T(8,128)(2,1)S(1)}, u32[]{:S(2)}, u32[]{:S(2)}) collective-permute-start(bf16[1,34,256]{2,1,0:T(8,128)(2,1)S(1)} %pad_maximum_fusion.6), channel_id=1, source_target_pairs={{0,8},{8,16},{16,24},{24,32},{32,40},{40,48},{48,56},{56,64},{64,7... | collective-permute-start | bytes 52232 | tf_op jit(solution)/shard_map/ppermute | solution.py:19
  18.9 3.4 %collective-permute-start.3 = (bf16[1,34,256]{2,1,0:T(8,128)(2,1)S(1)}, bf16[1,34,256]{2,1,0:T(8,128)(2,1)S(1)}, u32[]{:S(2)}, u32[]{:S(2)}) collective-permute-start(bf16[1,34,256]{2,1,0:T(8,128)(2,1)S(1)} %get-tuple-element.6), channel_id=1, source_target_pairs={{8,0},{16,8},{24,16},{32,24},{40,32},{48,40},{56,48},{64,56},{72,6... | collective-permute-start | bytes 52232 | tf_op jit(solution)/shard_map/ppermute | solution.py:21
  23.4 12.4 %collective-permute-start.5 = (bf16[18,34,256]{2,1,0:T(8,128)(2,1)S(1)}, bf16[18,34,256]{2,1,0:T(8,128)(2,1)S(1)}, u32[]{:S(2)}, u32[]{:S(2)}) collective-permute-start(bf16[18,34,256]{2,1,0:T(8,128)(2,1)S(1)} %get-tuple-element.20), channel_id=1, source_target_pairs={{0,8},{8,16},{16,24},{24,32},{32,40},{40,48},{48,56},{56,64},{64,7... | collective-permute-start | bytes 940040 | tf_op jit(solution)/shard_map/ppermute | solution.py:31
  25.4 14.3 %collective-permute-start.4 = (bf16[18,34,256]{2,1,0:T(8,128)(2,1)S(1)}, bf16[18,34,256]{2,1,0:T(8,128)(2,1)S(1)}, u32[]{:S(2)}, u32[]{:S(2)}) collective-permute-start(bf16[18,34,256]{2,1,0:T(8,128)(2,1)S(1)} %get-tuple-element.20), channel_id=1, source_target_pairs={{0,16},{8,24},{16,32},{24,40},{32,48},{40,56},{48,64},{56,72},{64,... | collective-permute-start | bytes 940040 | tf_op jit(solution)/shard_map/ppermute | solution.py:31
  30.7 15.9 %collective-permute-start.6 = (bf16[18,34,256]{2,1,0:T(8,128)(2,1)S(1)}, bf16[18,34,256]{2,1,0:T(8,128)(2,1)S(1)}, u32[]{:S(2)}, u32[]{:S(2)}) collective-permute-start(bf16[18,34,256]{2,1,0:T(8,128)(2,1)S(1)} %get-tuple-element.20), channel_id=1, source_target_pairs={{8,0},{16,8},{24,16},{32,24},{40,32},{48,40},{56,48},{64,56},{72,6... | collective-permute-start | bytes 940040 | tf_op jit(solution)/shard_map/ppermute | solution.py:31
  32.7 20.7 %collective-permute-start.7 = (bf16[18,34,256]{2,1,0:T(8,128)(2,1)S(1)}, bf16[18,34,256]{2,1,0:T(8,128)(2,1)S(1)}, u32[]{:S(2)}, u32[]{:S(2)}) collective-permute-start(bf16[18,34,256]{2,1,0:T(8,128)(2,1)S(1)} %get-tuple-element.20), channel_id=1, source_target_pairs={{16,0},{24,8},{32,16},{40,24},{48,32},{56,40},{64,48},{72,56},{80,... | collective-permute-start | bytes 940040 | tf_op jit(solution)/shard_map/ppermute | solution.py:31
  70.1 11.4 %collective-permute-start.8 = (bf16[1024,256]{0,1:T(8,128)(2,1)S(1)}, bf16[1024,256]{0,1:T(8,128)(2,1)S(1)}, u32[]{:S(2)}, u32[]{:S(2)}) collective-permute-start(bf16[1024,256]{0,1:T(8,128)(2,1)S(1)} %get-tuple-element.7), channel_id=1, source_target_pairs={{7,0},{0,1},{1,2},{2,3},{3,4},{4,5},{5,6},{6,7},{15,8},{8,9},{9,10... | collective-permute-start | bytes 1572872 | tf_op jit(solution)/shard_map/ppermute | solution.py:37
  70.1 15.0 %collective-permute-start.9 = (bf16[1024,256]{0,1:T(8,128)(2,1)S(1)}, bf16[1024,256]{0,1:T(8,128)(2,1)S(1)}, u32[]{:S(2)}, u32[]{:S(2)}) collective-permute-start(bf16[1024,256]{0,1:T(8,128)(2,1)S(1)} %get-tuple-element.8), channel_id=1, source_target_pairs={{1,0},{2,1},{3,2},{4,3},{5,4},{6,5},{7,6},{0,7},{9,8},{10,9},{11,1... | collective-permute-start | bytes 1572872 | tf_op jit(solution)/shard_map/ppermute | solution.py:37
where the time goes:
time: 86.9 us; the launch traced here: 86.4 us
  waiting for transfers between devices  39.7 us (46%)
  starting transfers between devices  21.2 us (24%)
  local copies, waits for them, and re-layouts  9.8 us (11%)
  matrix products  9.06 us (10%)
  other arithmetic  5.81 us (7%)
  between operations  0.9 us (1%)
    ppermute x4, waiting for transfers between devices, from_behind(): return lax.ppermute(block, axis, route)  15.8 us
    ppermute x2, waiting for transfers between devices, passed_along(): return lax.ppermute(block, axis, route)  13 us
    ppermute x4, starting transfers between devices, from_behind(): return lax.ppermute(block, axis, route)  12 us
    dot_general x1, matrix products, body(): jnp.dot(weights[0, 0], picked, preferred_element_type=jnp.float32)  9.06 us
    ppermute x2, waiting for transfers between devices, extended(): lax.ppermute(head, axis, [((i + 1) % count, i) for i in range(ends)])  7.35 us
    ppermute x2, starting transfers between devices, extended(): lax.ppermute(tail, axis, [(i, (i + 1) % count) for i in range(ends)])  5.1 us
    unnamed x6, local copies, waits for them, and re-layouts  3.76 us
    ppermute x2, waiting for transfers between devices, extended(): lax.ppermute(tail, axis, [(i, (i + 1) % count) for i in range(ends)])  3.53 us
  transfers between devices with their start and end apart: 10, of which 9 were waited for; matrix products, arithmetic and copies ran while one was open for 4% of the time, Pallas kernels for 0%

commit v1 on v0

v1 whole, which is shorter than its diff:
```python
import functools

import jax
import jax.numpy as jnp
from jax import lax
from jax.experimental import pallas as pl
from jax.experimental.pallas import tpu as pltpu
from jax.sharding import PartitionSpec as P

MESH = pl.DeviceIdType.MESH
F32 = jnp.float32
BF16 = jnp.bfloat16

ROWS = 16
LON = 32
CHAN = 256
STRIP_ROWS = 4
SLOTS = 8
CELLS = STRIP_ROWS * LON
DEPTH = 3 * CELLS
TGT = 1024
PARTS = 1
WIDTH = CHAN // PARTS
STEP = 256
STEPS = TGT // STEP
W_COPIES = 12
PIECES = 5


def kernel(
    ids_ref, counts_ref, field_ref, w_ref, out_ref,
    nb, rims, edge_out, edge_in, x_ref, w_vmem, centre, to_east, to_west, from_west, from_east,
    field_sem, w_sem,
    p_send, p_recv, z_send, z_recv, d_send, d_recv, f_send, f_recv, e_send, e_recv, r_send, r_recv,
    b_send, b_recv,
):
    lat = lax.axis_index("lat")
    lon = lax.axis_index("lon")
    core = lat % 2
    y_lo = (lat // 2) % 2
    sibling = lat + 1 - 2 * core
    partner = lat + 2 - 4 * y_lo
    relay_to = (lat + 4 - 8 * y_lo + 16) % 16
    relay_from = (lat - 4 + 8 * y_lo + 16) % 16
    above3 = (lat + 13) % 16
    below3 = (lat + 3) % 16
    east = (lon + 1) % 8
    west = (lon + 7) % 8

    def device(a, o):
        return (a, o)

    own = 1 + 2 * ROWS
    field_copies = []
    for h in range(PARTS):
        field_copies.append(
            pltpu.make_async_copy(
                field_ref.at[:, :, pl.ds(h * WIDTH, WIDTH)], nb.at[h, pl.ds(own, ROWS)], field_sem.at[h]
            )
        )
        field_copies[-1].start()

    barrier = pltpu.get_barrier_semaphore()
    peers = (
        (above3, lon), (below3, lon), (lat, east), (lat, west),
        (relay_to, lon), (relay_from, lon), (partner, lon), (sibling, lon),
    )
    for peer in peers:
        pl.semaphore_signal(barrier, inc=1, device_id=peer, device_id_type=MESH)

    w_rows = 3 * TGT // W_COPIES
    w_copies = []
    for i in range(W_COPIES):
        rows = pl.ds(i * w_rows, w_rows)
        w_copies.append(pltpu.make_async_copy(w_ref.at[0, 0, rows], w_vmem.at[rows], w_sem.at[i]))
        w_copies[-1].start()

    for copy in field_copies:
        copy.wait()
    row8 = lax.broadcasted_iota(jnp.int32, (8, WIDTH), 0)
    for h in range(PARTS):
        for q in range(4):
            first = jnp.zeros((8, WIDTH), F32)
            last = jnp.zeros((8, WIDTH), F32)
            for i in range(4):
                head = nb[h, own + 4 * q + i, 0:16].astype(F32)
                tail = nb[h, own + 4 * q + i, LON - 16 : LON].astype(F32)
                first = jnp.where(row8 == 4 + i, jnp.broadcast_to(head[0:1], (8, WIDTH)), first)
                last = jnp.where(row8 == i, jnp.broadcast_to(tail[15:16], (8, WIDTH)), last)
            edge_out[h, 0, q] = first.astype(BF16)
            edge_out[h, 1, q] = last.astype(BF16)

    pl.semaphore_wait(barrier, len(peers))

    pending = []

    def send(src, dst, send_sem, recv_sem, peer):
        copy = pltpu.make_async_remote_copy(
            src_ref=src, dst_ref=dst, send_sem=send_sem, recv_sem=recv_sem,
            device_id=peer, device_id_type=MESH,
        )
        copy.start()
        return copy

    def piece(h, slot, n):
        if n == PIECES - 1:
            return nb.at[h, pl.ds(1 + ROWS * slot + 12, 4)]
        if n == PIECES - 2:
            return rims.at[h, pl.ds(4 * slot, 4)]
        return nb.at[h, pl.ds(1 + ROWS * slot + 4 * n, 4)]

    def piece_copy(src, dst, send_sem, recv_sem, peer):
        return pltpu.make_async_remote_copy(
            src_ref=src, dst_ref=dst, send_sem=send_sem, recv_sem=recv_sem,
            device_id=peer, device_id_type=MESH,
        )

    p_slot = 4 * (1 - y_lo)
    q_slot = 4 * y_lo
    fwd_src = 4 * (1 - core)
    fwd_dst = 3 - 2 * core
    own_dst = 1 + 2 * core

    def p_copy(h, n):
        return piece_copy(piece(h, 2, n), piece(h, q_slot, n), p_send.at[h, n], p_recv.at[h, n], (partner, lon))

    def z_copy(h, n):
        return piece_copy(piece(h, p_slot, n), piece(h, q_slot, n), z_send.at[h, n], z_recv.at[h, n], (relay_to, lon))

    def d_copy(h, n):
        return piece_copy(piece(h, 2, n), piece(h, own_dst, n), d_send.at[h, n], d_recv.at[h, n], (sibling, lon))

    def f_copy(h, n):
        return piece_copy(piece(h, fwd_src, n), piece(h, fwd_dst, n), f_send.at[h, n], f_recv.at[h, n], (sibling, lon))

    def e_copies(h):
        return (
            piece_copy(edge_out.at[h, 0], edge_in.at[h, 0], e_send.at[h, 0], e_recv.at[h, 0], (lat, west)),
            piece_copy(edge_out.at[h, 1], edge_in.at[h, 1], e_send.at[h, 1], e_recv.at[h, 1], (lat, east)),
        )

    def r_copies(h):
        return (
            piece_copy(nb.at[h, pl.ds(own, 1)], nb.at[h, pl.ds(1 + 5 * ROWS, 1)], r_send.at[h, 0], r_recv.at[h, 0], (above3, lon)),
            piece_copy(nb.at[h, pl.ds(own + ROWS - 1, 1)], nb.at[h, pl.ds(0, 1)], r_send.at[h, 1], r_recv.at[h, 1], (below3, lon)),
        )

    for h in range(PARTS):
        for copy in e_copies(h):
            copy.start()
        for n in range(3):
            p_copy(h, n).start()
            d_copy(h, n).start()
        for copy in r_copies(h):
            copy.start()
    for h in range(PARTS):
        for copy in e_copies(h):
            copy.wait_recv()
        rims[h, 8:12] = edge_in[h, 0] + edge_in[h, 1]
        for n in (3, 4):
            p_copy(h, n).start()
            d_copy(h, n).start()

    def on_p(h, n):
        p_copy(h, n).wait_recv()
        z_copy(h, n).start()

        @pl.when(core == y_lo)
        def _():
            f_copy(h, n).start()

    def on_q(h, n):
        z_copy(h, n).wait_recv()

        @pl.when(core != y_lo)
        def _():
            f_copy(h, n).start()

    for h in range(PARTS):
        for n in range(PIECES):
            on_p(h, n)
            if n > 0:
                on_q(h, n - 1)
        on_q(h, PIECES - 1)

    column = lax.broadcasted_iota(jnp.int32, (LON, WIDTH), 0)

    def stencil(h):
        def slot(k, carry):
            strip = jnp.clip(ids_ref[0, k] - (lat - 2) * 4, 0, 19)
            live = k < counts_ref[0]
            base = strip * 4
            rim = rims[h, strip].astype(F32)
            rows = [nb[h, base + i].astype(F32) for i in range(6)]
            top = (lat - 2) * ROWS + base
            rows[0] = jnp.where(top == 0, rows[1], rows[0])
            rows[5] = jnp.where(top == 256 - STRIP_ROWS, rows[4], rows[5])
            at = k * DEPTH
            for i in range(4):
                centre_row = rows[i + 1]
                before = jnp.where(column == 0, jnp.broadcast_to(rim[i : i + 1], (LON, WIDTH)), pltpu.roll(centre_row, 1, 0))
                after = jnp.where(
                    column == LON - 1, jnp.broadcast_to(rim[4 + i : 5 + i], (LON, WIDTH)), pltpu.roll(centre_row, LON - 1, 0)
                )
                values = (centre_row, (after - before) * 0.5, (rows[i + 2] - rows[i]) * 0.5)
                for part, value in enumerate(values):
                    kept = jnp.where(live, value, jnp.zeros_like(value)).astype(BF16)
                    x_ref[h, pl.ds(pl.multiple_of(at + part * CELLS + i * LON, LON), LON)] = kept
            return carry

        lax.fori_loop(0, SLOTS, slot, 0)

    def b_copy(h, side, i, rows):
        src, dst, peer = (
            (to_east, from_west, (lat, east)) if side == 0 else (to_west, from_east, (lat, west))
        )
        return piece_copy(src.at[h, rows], dst.at[h, rows], b_send.at[h, side, i], b_recv.at[h, side, i], peer)

    for h in range(PARTS):
        if h == 0:
            for copy in w_copies:
                copy.wait()
        for n in range(PIECES):
            d_copy(h, n).wait_recv()
            f_copy(h, n).wait_recv()
        for copy in r_copies(h):
            copy.wait_recv()
        stencil(h)

        def outward(i, carry):
            at = pl.multiple_of(i * STEP, STEP)
            rows = pl.ds(at, STEP)
            for side, base, dst in ((0, 2 * TGT, to_east), (1, 0, to_west)):
                part = jnp.dot(w_vmem[pl.ds(base + at, STEP)], x_ref[h], preferred_element_type=F32)
                dst[h, rows] = part.astype(BF16)
                b_copy(h, side, i, rows).start()
            return carry

        lax.fori_loop(0, STEPS, outward, 0)

        def inward(i, carry):
            at = pl.multiple_of(i * STEP, STEP)
            rows = pl.ds(at, STEP)
            centre[h, rows] = jnp.dot(w_vmem[pl.ds(TGT + at, STEP)], x_ref[h], preferred_element_type=F32)
            return carry

        lax.fori_loop(0, STEPS, inward, 0)

    for h in range(PARTS):

        def finish(i, carry):
            at = pl.multiple_of(i * STEP, STEP)
            rows = pl.ds(at, STEP)
            for side in range(2):
                b_copy(h, side, i, rows).wait_recv()
            total = centre[h, rows] + from_west[h, rows].astype(F32) + from_east[h, rows].astype(F32)
            out_ref[rows, h * WIDTH : (h + 1) * WIDTH] = total.astype(BF16)
            return carry

        lax.fori_loop(0, STEPS, finish, 0)

    for h in range(PARTS):
        for n in range(PIECES):
            p_copy(h, n).wait_send()
            z_copy(h, n).wait_send()
            d_copy(h, n).wait_send()
            f_copy(h, n).wait_send()
        for copy in e_copies(h) + r_copies(h):
            copy.wait_send()

        def sent(i, carry):
            rows = pl.ds(pl.multiple_of(i * STEP, STEP), STEP)
            for side in range(2):
                b_copy(h, side, i, rows).wait_send()
            return carry

        lax.fori_loop(0, STEPS, sent, 0)


def body(field, weights, strip_ids, counts):
    dma = pltpu.SemaphoreType.DMA
    return pl.pallas_call(
        kernel,
        out_shape=jax.ShapeDtypeStruct((TGT, CHAN), BF16),
        in_specs=[
            pl.BlockSpec(memory_space=pltpu.SMEM),
            pl.BlockSpec(memory_space=pltpu.SMEM),
            pl.BlockSpec(memory_space=pltpu.HBM),
            pl.BlockSpec(memory_space=pltpu.HBM),
        ],
        out_specs=pl.BlockSpec(memory_space=pltpu.VMEM),
        scratch_shapes=[
            pltpu.VMEM((PARTS, 5 * ROWS + 2, LON, WIDTH), BF16),
            pltpu.VMEM((PARTS, 20, 8, WIDTH), BF16),
            pltpu.VMEM((PARTS, 2, 4, 8, WIDTH), BF16),
            pltpu.VMEM((PARTS, 2, 4, 8, WIDTH), BF16),
            pltpu.VMEM((PARTS, SLOTS * DEPTH, WIDTH), BF16),
            pltpu.VMEM((3 * TGT, SLOTS * DEPTH), BF16),
            pltpu.VMEM((PARTS, TGT, WIDTH), F32),
            pltpu.VMEM((PARTS, TGT, WIDTH), BF16),
            pltpu.VMEM((PARTS, TGT, WIDTH), BF16),
            pltpu.VMEM((PARTS, TGT, WIDTH), BF16),
            pltpu.VMEM((PARTS, TGT, WIDTH), BF16),
            dma((PARTS,)),
            dma((W_COPIES,)),
            dma((PARTS, PIECES)), dma((PARTS, PIECES)),
            dma((PARTS, PIECES)), dma((PARTS, PIECES)),
            dma((PARTS, PIECES)), dma((PARTS, PIECES)),
            dma((PARTS, PIECES)), dma((PARTS, PIECES)),
            dma((PARTS, 2)), dma((PARTS, 2)),
            dma((PARTS, 2)), dma((PARTS, 2)),
            dma((PARTS, 2, STEPS)), dma((PARTS, 2, STEPS)),
        ],
        compiler_params=pltpu.CompilerParams(
            collective_id=0, has_side_effects=True, vmem_limit_bytes=48 * 1024 * 1024
        ),
    )(strip_ids, counts, field, weights)


def solution(mesh):
    placed = (P("lat", "lon", None), P("lat", "lon", None, None), P("lat", None), P("lat"))
    return jax.shard_map(
        body, mesh=mesh, in_specs=placed, out_specs=P(("lat", "lon"), None), check_vma=False
    )
```

time: 86.9 us -> 43.3 us (0.50)
  the two profiles are of different devices: /device:TPU:38 before, /device:TPU:9 now
where the time goes in v1:
time: 43.3 us; the launch traced here: 43.2 us
  Pallas kernels  40.1 us (93%)
  local copies, waits for them, and re-layouts  2.39 us (6%)
  between operations  0.67 us (2%)
    pallas_call x1, Pallas kernels, body(): pl.pallas_call(kernel, out_shape=jax.ShapeDtypeStruct((TGT, CHAN), BF16),...  40.1 us
    unnamed x5, local copies, waits for them, and re-layouts  2.39 us

profile of v1, /device:TPU:9, one launch (start us, length us, event | category | flops | bytes accessed | tf_op | source)
XLA Modules:
  0.0 43.2 jit_solution(11536585369003920927)
XLA Ops:
  0.7 0.0 copy-start
  0.7 0.9 %copy-done = bf16[16,32,256]{2,1,0:T(8,128)(2,1)S(1)} copy-done((bf16[16,32,256]{2,1,0:T(8,128)(2,1)S(1)}, bf16[16,32,256]{2,1,0:T(8,128)(2,1)}, u32[]{:S(2)}) %copy-start) | copy-done | bytes 262168
  1.6 0.0 copy-start.1
  1.6 0.7 %copy-done.1 = s32[1,8]{1,0:T(1,128)S(1)} copy-done((s32[1,8]{1,0:T(1,128)S(1)}, s32[1,8]{1,0:T(1,128)}, u32[]{:S(2)}) %copy-start.1) | copy-done | bytes 56
  2.3 40.1 %shard_map.46 = bf16[1024,256]{1,0:T(8,128)(2,1)S(1)} custom-call(s32[1,8]{1,0:T(1,128)S(1)} %copy-done.1, s32[1]{0:T(128)S(6)} %copy.6.counts_ref, bf16[16,32,256]{2,1,0:T(8,128)(2,1)S(1)} %copy-done, bf16[1,1,3072,3072]{3,2,1,0:T(8,128)(2,1)} %w_ref.1), custom_call_target="tpu_custom_call" | custom-call | tf_op jit(solution)/shard_map/pallas_call | solution.py:282
  42.4 0.8 %copy.7 = bf16[1024,256]{1,0:T(8,128)(2,1)} copy(bf16[1024,256]{1,0:T(8,128)(2,1)S(1)} %shard_map.46) | data formatting | bytes 1048576
Async XLA Ops:
  0.7 1.0 %copy-start = (bf16[16,32,256]{2,1,0:T(8,128)(2,1)S(1)}, bf16[16,32,256]{2,1,0:T(8,128)(2,1)}, u32[]{:S(2)}) copy-start(bf16[16,32,256]{2,1,0:T(8,128)(2,1)} %field_ref.1) | copy-start | bytes 786436
  1.6 0.7 %copy-start.1 = (s32[1,8]{1,0:T(1,128)S(1)}, s32[1,8]{1,0:T(1,128)}, u32[]{:S(2)}) copy-start(s32[1,8]{1,0:T(1,128)} %ids_ref.1) | copy-start | bytes 100

commit v2 on v1

v2 whole, which is shorter than its diff:
```python
import jax
import jax.numpy as jnp
from jax import lax
from jax.experimental import pallas as pl
from jax.experimental.pallas import tpu as pltpu
from jax.sharding import PartitionSpec as P

MESH = pl.DeviceIdType.MESH
F32 = jnp.float32
BF16 = jnp.bfloat16

N_LAT = 16
N_LON = 8
ROWS = 16
LON = 32
CHAN = 256
STRIP_ROWS = 4
SLOTS = 8
CELLS = STRIP_ROWS * LON
DEPTH = 3 * CELLS
TGT = 1024
PARTS = 2
WIDTH = CHAN // PARTS
STEP = 256
STEPS = TGT // STEP
W_COPIES = 12
PIECES = 4
OWN = 1 + 2 * ROWS
NEAR = (-2, -1, 1, 2)


def kernel(
    ids_hbm, counts_hbm, field_ref, w_ref, out_ref,
    ids_ref, counts_ref, nb_first, nb_second, rims, edge_out, edge_in, x_ref, w_vmem, centre,
    to_east, to_west, from_west, from_east,
    field_sem, w_sem, ids_sem,
    p_send, p_recv, z_send, z_recv, d_send, d_recv, f_send, f_recv,
    e_send, e_recv, m_send, m_recv, r_send, r_recv, b_send, b_recv,
):
    nb = (nb_first, nb_second)
    lat = lax.axis_index("lat")
    lon = lax.axis_index("lon")
    core = lat % 2
    y_lo = (lat // 2) % 2
    sibling = lat + 1 - 2 * core
    partner = lat + 2 - 4 * y_lo
    relay_to = lat + 4 - 8 * y_lo
    relay_from = lat - 4 + 8 * y_lo
    east = (lon + 1) % N_LON
    west = (lon + N_LON - 1) % N_LON

    def inside(a):
        return (a >= 0) & (a < N_LAT)

    has_relay_to = inside(relay_to)
    has_relay_from = inside(relay_from)

    field_copies = [
        pltpu.make_async_copy(
            field_ref.at[:, :, pl.ds(h * WIDTH, WIDTH)], nb[h].at[pl.ds(OWN, ROWS)], field_sem.at[h]
        )
        for h in range(PARTS)
    ]
    for copy in field_copies:
        copy.start()
    id_copies = (
        pltpu.make_async_copy(ids_hbm, ids_ref, ids_sem.at[0]),
        pltpu.make_async_copy(counts_hbm, counts_ref, ids_sem.at[1]),
    )
    for copy in id_copies:
        copy.start()

    barrier = pltpu.get_barrier_semaphore()
    for peer in (east, west):
        pl.semaphore_signal(barrier, inc=1, device_id=(lat, peer), device_id_type=MESH)
    arrivals = 2
    for d in (-4, 4, -3, 3, -2, 2, -1, 1):

        @pl.when(inside(lat + d))
        def _(d=d):
            pl.semaphore_signal(barrier, inc=1, device_id=(lat + d, lon), device_id_type=MESH)

        arrivals = arrivals + jnp.where(inside(lat + d), 1, 0)

    w_rows = 3 * TGT // W_COPIES
    w_copies = []
    for i in range(W_COPIES):
        rows = pl.ds(i * w_rows, w_rows)
        w_copies.append(pltpu.make_async_copy(w_ref.at[0, 0, rows], w_vmem.at[rows], w_sem.at[i]))
        w_copies[-1].start()

    for copy in field_copies:
        copy.wait()
    row8 = lax.broadcasted_iota(jnp.int32, (8, WIDTH), 0)
    for h in range(PARTS):
        for q in range(4):
            first = jnp.zeros((8, WIDTH), F32)
            last = jnp.zeros((8, WIDTH), F32)
            for i in range(4):
                head = nb[h][OWN + 4 * q + i, 0:16].astype(F32)
                tail = nb[h][OWN + 4 * q + i, LON - 16 : LON].astype(F32)
                first = jnp.where(row8 == 4 + i, jnp.broadcast_to(head[0:1], (8, WIDTH)), first)
                last = jnp.where(row8 == i, jnp.broadcast_to(tail[15:16], (8, WIDTH)), last)
            edge_out[0, q, h] = first.astype(BF16)
            edge_out[1, q, h] = last.astype(BF16)

    with jax.named_scope("barrier"):
        pl.semaphore_wait(barrier, arrivals)

    def remote(src, dst, send_sem, recv_sem, peer):
        return pltpu.make_async_remote_copy(
            src_ref=src, dst_ref=dst, send_sem=send_sem, recv_sem=recv_sem,
            device_id=peer, device_id_type=MESH,
        )

    def piece(h, slot, n):
        return nb[h].at[pl.ds(1 + ROWS * slot + 4 * n, 4)]

    p_slot = 4 * (1 - y_lo)
    q_slot = 4 * y_lo
    fwd_src = 4 * (1 - core)
    fwd_dst = 3 - 2 * core
    own_dst = 1 + 2 * core

    def p_copy(h, n):
        return remote(piece(h, 2, n), piece(h, q_slot, n), p_send.at[h, n], p_recv.at[h, n], (partner, lon))

    def z_copy(h, n):
        return remote(piece(h, p_slot, n), piece(h, q_slot, n), z_send.at[h, n], z_recv.at[h, n], (relay_to, lon))

    def d_copy(h, n):
        return remote(piece(h, 2, n), piece(h, own_dst, n), d_send.at[h, n], d_recv.at[h, n], (sibling, lon))

    def f_copy(h, n):
        return remote(piece(h, fwd_src, n), piece(h, fwd_dst, n), f_send.at[h, n], f_recv.at[h, n], (sibling, lon))

    e_copies = (
        remote(edge_out.at[0], edge_in.at[0], e_send.at[0], e_recv.at[0], (lat, west)),
        remote(edge_out.at[1], edge_in.at[1], e_send.at[1], e_recv.at[1], (lat, east)),
    )

    def m_copy(d):
        slot = 2 - d
        return remote(
            rims.at[pl.ds(8, 4)], rims.at[pl.ds(4 * slot, 4)], m_send.at[slot], m_recv.at[slot], (lat + d, lon)
        )

    def up_copy(h):
        src, dst = nb[h].at[pl.ds(OWN, 1)], nb[h].at[pl.ds(1 + 5 * ROWS, 1)]
        return remote(src, dst, r_send.at[h, 0], r_recv.at[h, 0], (lat - 3, lon))

    def down_copy(h):
        src, dst = nb[h].at[pl.ds(OWN + ROWS - 1, 1)], nb[h].at[pl.ds(0, 1)]
        return remote(src, dst, r_send.at[h, 1], r_recv.at[h, 1], (lat + 3, lon))

    for copy in e_copies:
        copy.start()
    def send_own(h):
        for n in range(PIECES):
            p_copy(h, n).start()
            d_copy(h, n).start()
        pl.when(inside(lat - 3))(lambda: up_copy(h).start())
        pl.when(inside(lat + 3))(lambda: down_copy(h).start())

    send_own(0)

    has_fwd_out = ((core == 0) & (lat < 14)) | ((core == 1) & (lat >= 2))
    has_fwd_in = ((core == 1) & (lat < 14)) | ((core == 0) & (lat >= 2))

    def on_p(h, n):
        p_copy(h, n).wait_recv()
        pl.when(has_relay_to)(lambda: z_copy(h, n).start())
        pl.when(core == y_lo)(lambda: f_copy(h, n).start())

    def on_q(h):
        @pl.when(has_relay_from)
        def _():
            for n in range(PIECES):
                z_copy(h, n).wait_recv()
                pl.when(core != y_lo)(lambda n=n: f_copy(h, n).start())

    def tiles_in(h):
        for n in range(PIECES):
            d_copy(h, n).wait_recv()
        pl.when(inside(lat + 3))(lambda: up_copy(h).wait_recv())
        pl.when(inside(lat - 3))(lambda: down_copy(h).wait_recv())

        @pl.when(has_fwd_in)
        def _():
            for n in range(PIECES):
                f_copy(h, n).wait_recv()

    column = lax.broadcasted_iota(jnp.int32, (LON, WIDTH), 0)

    def stencil(h):
        def slot(k, carry):
            strip = jnp.clip(ids_ref[0, k] - (lat - 2) * 4, 0, 19)
            live = k < counts_ref[0]
            base = strip * 4
            rim = rims[strip, h].astype(F32)
            rows = [nb[h][base + i].astype(F32) for i in range(6)]
            top = (lat - 2) * ROWS + base
            rows[0] = jnp.where(top == 0, rows[1], rows[0])
            rows[5] = jnp.where(top == N_LAT * ROWS - STRIP_ROWS, rows[4], rows[5])
            at = k * DEPTH
            for i in range(4):
                mid = rows[i + 1]
                before = jnp.where(column == 0, jnp.broadcast_to(rim[i : i + 1], (LON, WIDTH)), pltpu.roll(mid, 1, 0))
                after = jnp.where(
                    column == LON - 1, jnp.broadcast_to(rim[4 + i : 5 + i], (LON, WIDTH)), pltpu.roll(mid, LON - 1, 0)
                )
                values = (mid, (after - before) * 0.5, (rows[i + 2] - rows[i]) * 0.5)
                for part, value in enumerate(values):
                    kept = jnp.where(live, value, jnp.zeros_like(value)).astype(BF16)
                    cells = pl.ds(pl.multiple_of(at + part * CELLS + i * LON, LON), LON)
                    x_ref[cells, h * WIDTH : (h + 1) * WIDTH] = kept
            return carry

        with jax.named_scope("stencil"):
            lax.fori_loop(0, SLOTS, slot, 0)

    def b_copy(h, side, i):
        rows = pl.ds(i * STEP, STEP)
        if side == 0:
            return remote(to_east.at[h, rows], from_west.at[h, rows], b_send.at[h, 0, i], b_recv.at[h, 0, i], (lat, east))
        return remote(to_west.at[h, rows], from_east.at[h, rows], b_send.at[h, 1, i], b_recv.at[h, 1, i], (lat, west))

    def outward(h, i):
        with jax.named_scope("outward"):
            at = i * STEP
            x = x_ref[:, h * WIDTH : (h + 1) * WIDTH]
            for_east = jnp.dot(w_vmem[pl.ds(2 * TGT + at, STEP)], x, preferred_element_type=F32)
            for_west = jnp.dot(w_vmem[pl.ds(at, STEP)], x, preferred_element_type=F32)
            to_east[h, pl.ds(at, STEP)] = for_east.astype(BF16)
            to_west[h, pl.ds(at, STEP)] = for_west.astype(BF16)
            b_copy(h, 0, i).start()
            b_copy(h, 1, i).start()

    with jax.named_scope("relay0"):
        on_p(0, 0)
        on_p(0, 1)
        for copy in e_copies:
            copy.wait_recv()
        rims[8:12] = edge_in[0] + edge_in[1]
        for d in NEAR:
            pl.when(inside(lat + d))(lambda d=d: m_copy(d).start())
        send_own(1)
        for n in range(2, PIECES):
            on_p(0, n)
    with jax.named_scope("q0"):
        on_q(0)
    with jax.named_scope("weights"):
        for copy in (*w_copies, *id_copies):
            copy.wait()
    with jax.named_scope("rims"):
        for d in NEAR:
            pl.when(inside(lat - d))(lambda d=d: m_copy(d).wait_recv())
    with jax.named_scope("tiles0"):
        tiles_in(0)
    stencil(0)
    outward(0, 0)
    for h in range(1, PARTS):
        with jax.named_scope("p1"):
            for n in range(PIECES):
                on_p(h, n)
        outward(h - 1, 1)
        outward(h - 1, 2)
        with jax.named_scope("q1"):
            on_q(h)
        outward(h - 1, 3)
        with jax.named_scope("tiles1"):
            tiles_in(h)
        stencil(h)
        outward(h, 0)
    for i in range(1, STEPS):
        outward(PARTS - 1, i)
    with jax.named_scope("inward"):
        half = TGT // 2
        x = x_ref[...]
        upper = jnp.dot(w_vmem[pl.ds(TGT, half)], x, preferred_element_type=F32)
        lower = jnp.dot(w_vmem[pl.ds(TGT + half, half)], x, preferred_element_type=F32)
        centre[:half] = upper
        centre[half:] = lower

    for h in range(PARTS):
        columns = pl.ds(h * WIDTH, WIDTH)
        for i in range(STEPS):
            with jax.named_scope("finish"):
                rows = pl.ds(i * STEP, STEP)
                for side in range(2):
                    b_copy(h, side, i).wait_recv()
                total = centre[rows, columns] + from_west[h, rows].astype(F32) + from_east[h, rows].astype(F32)
                out_ref[rows, columns] = total.astype(BF16)

    with jax.named_scope("tail"):
        for h in range(PARTS):
            for n in range(PIECES):
                p_copy(h, n).wait_send()
                d_copy(h, n).wait_send()
                pl.when(has_relay_to)(lambda h=h, n=n: z_copy(h, n).wait_send())
                pl.when(has_fwd_out)(lambda h=h, n=n: f_copy(h, n).wait_send())
            for i in range(STEPS):
                for side in range(2):
                    b_copy(h, side, i).wait_send()
        for copy in e_copies:
            copy.wait_send()
        for d in NEAR:
            pl.when(inside(lat + d))(lambda d=d: m_copy(d).wait_send())
        for h in range(PARTS):
            pl.when(inside(lat - 3))(lambda h=h: up_copy(h).wait_send())
            pl.when(inside(lat + 3))(lambda h=h: down_copy(h).wait_send())


def body(field, weights, strip_ids, counts):
    dma = pltpu.SemaphoreType.DMA
    field, weights, strip_ids = (
        pltpu.with_memory_space_constraint(a, pltpu.HBM) for a in (field, weights, strip_ids)
    )
    return pl.pallas_call(
        kernel,
        out_shape=jax.ShapeDtypeStruct((TGT, CHAN), BF16),
        in_specs=[pl.BlockSpec(memory_space=pl.ANY)] * 4,
        out_specs=pl.BlockSpec(memory_space=pltpu.VMEM),
        scratch_shapes=[
            pltpu.SMEM((1, SLOTS), jnp.int32),
            pltpu.SMEM((1,), jnp.int32),
            pltpu.VMEM((5 * ROWS + 2, LON, WIDTH), BF16),
            pltpu.VMEM((5 * ROWS + 2, LON, WIDTH), BF16),
            pltpu.VMEM((20, PARTS, 8, WIDTH), BF16),
            pltpu.VMEM((2, 4, PARTS, 8, WIDTH), BF16),
            pltpu.VMEM((2, 4, PARTS, 8, WIDTH), BF16),
            pltpu.VMEM((SLOTS * DEPTH, CHAN), BF16),
            pltpu.VMEM((3 * TGT, SLOTS * DEPTH), BF16),
            pltpu.VMEM((TGT, CHAN), F32),
            pltpu.VMEM((PARTS, TGT, WIDTH), BF16),
            pltpu.VMEM((PARTS, TGT, WIDTH), BF16),
            pltpu.VMEM((PARTS, TGT, WIDTH), BF16),
            pltpu.VMEM((PARTS, TGT, WIDTH), BF16),
            dma((PARTS,)), dma((W_COPIES,)), dma((2,)),
            dma((PARTS, PIECES)), dma((PARTS, PIECES)),
            dma((PARTS, PIECES)), dma((PARTS, PIECES)),
            dma((PARTS, PIECES)), dma((PARTS, PIECES)),
            dma((PARTS, PIECES)), dma((PARTS, PIECES)),
            dma((2,)), dma((2,)),
            dma((5,)), dma((5,)),
            dma((PARTS, 2)), dma((PARTS, 2)),
            dma((PARTS, 2, STEPS)), dma((PARTS, 2, STEPS)),
        ],
        compiler_params=pltpu.CompilerParams(
            collective_id=0, has_side_effects=True, vmem_limit_bytes=48 * 1024 * 1024
        ),
    )(strip_ids, counts, field, weights)


def solution(mesh):
    placed = (P("lat", "lon", None), P("lat", "lon", None, None), P("lat", None), P("lat"))
    return jax.shard_map(
        body, mesh=mesh, in_specs=placed, out_specs=P(("lat", "lon"), None), check_vma=False
    )
```

time: 43.3 us -> 36.4 us (0.84)
  Pallas kernels: 40.1 us -> 34.8 us
  local copies, waits for them, and re-layouts: 2.39 us -> 0.8 us
    pallas_call x1, Pallas kernels: 40.1 us -> 34.8 us  [body(): pl.pallas_call(kernel, out_shape=jax.ShapeDtypeStruct((TGT, CHAN), BF16),...]
    unnamed x5 -> x1, local copies, waits for them, and re-layouts: 2.39 us -> 0.8 us
where the time goes in v2:
time: 36.4 us; the launch traced here: 36.2 us
  Pallas kernels  34.8 us (96%)
  local copies, waits for them, and re-layouts  0.8 us (2%)
  between operations  0.66 us (2%)
    pallas_call x1, Pallas kernels, body(): pl.pallas_call(kernel, out_shape=jax.ShapeDtypeStruct((TGT, CHAN), BF16),...  34.8 us
    unnamed x1, local copies, waits for them, and re-layouts  0.8 us

profile of v2, /device:TPU:9, one launch (start us, length us, event | category | flops | bytes accessed | tf_op | source)
XLA Modules:
  0.0 36.2 jit_solution(2364049439173308023)
XLA Ops:
  0.7 34.8 %shard_map.46 = bf16[1024,256]{1,0:T(8,128)(2,1)S(1)} custom-call(s32[1,8]{1,0:T(1,128)} %ids_hbm.1, s32[1]{0:T(128)S(6)} %copy.6.counts_hbm, bf16[16,32,256]{2,1,0:T(8,128)(2,1)} %field_ref.1, bf16[1,1,3072,3072]{3,2,1,0:T(8,128)(2,1)} %w_ref.1), custom_call_target="tpu_custom_call" | custom-call | tf_op jit(solution)/shard_map/pallas_call | solution.py:319
  35.5 0.8 %copy.7 = bf16[1024,256]{1,0:T(8,128)(2,1)} copy(bf16[1024,256]{1,0:T(8,128)(2,1)S(1)} %shard_map.46) | data formatting | bytes 1048576

commit v3 on v2

--- a/solution.py
+++ b/solution.py
@@ -33,7 +33,7 @@
     ids_hbm, counts_hbm, field_ref, w_ref, out_ref,
     ids_ref, counts_ref, nb_first, nb_second, rims, edge_out, edge_in, x_ref, w_vmem, centre,
     to_east, to_west, from_west, from_east,
-    field_sem, w_sem, ids_sem,
+    field_sem, w_sem, ids_sem, ready_sem,
     p_send, p_recv, z_send, z_recv, d_send, d_recv, f_send, f_recv,
     e_send, e_recv, m_send, m_recv, r_send, r_recv, b_send, b_recv,
 ):
@@ -71,9 +71,17 @@
         copy.start()
 
     barrier = pltpu.get_barrier_semaphore()
-    for peer in (east, west):
-        pl.semaphore_signal(barrier, inc=1, device_id=(lat, peer), device_id_type=MESH)
-    arrivals = 2
+    x_pos = lon % 4
+    at_end = (x_pos == 0) | (x_pos == 3)
+    across_x = jnp.where(x_pos == 0, lon + 3, lon - 3)
+    across_y = (lon + 4) % N_LON
+    for valid, peer in ((x_pos != 3, east), (x_pos != 0, west), (at_end, across_x), (at_end, across_y)):
+
+        @pl.when(valid)
+        def _(peer=peer):
+            pl.semaphore_signal(barrier, inc=1, device_id=(lat, peer), device_id_type=MESH)
+
+    arrivals = jnp.where(at_end, 3, 2)
     for d in (-4, 4, -3, 3, -2, 2, -1, 1):
 
         @pl.when(inside(lat + d))
@@ -107,6 +115,10 @@
     with jax.named_scope("barrier"):
         pl.semaphore_wait(barrier, arrivals)
 
+    @pl.when(at_end)
+    def _():
+        pl.semaphore_signal(ready_sem, inc=1, device_id=(lat, across_y), device_id_type=MESH)
+
     def remote(src, dst, send_sem, recv_sem, peer):
         return pltpu.make_async_remote_copy(
             src_ref=src, dst_ref=dst, send_sem=send_sem, recv_sem=recv_sem,
@@ -153,8 +165,6 @@
         src, dst = nb[h].at[pl.ds(OWN + ROWS - 1, 1)], nb[h].at[pl.ds(0, 1)]
         return remote(src, dst, r_send.at[h, 1], r_recv.at[h, 1], (lat + 3, lon))
 
-    for copy in e_copies:
-        copy.start()
     def send_own(h):
         for n in range(PIECES):
             p_copy(h, n).start()
@@ -163,6 +173,15 @@
         pl.when(inside(lat + 3))(lambda: down_copy(h).start())
 
     send_own(0)
+    send_own(1)
+    with jax.named_scope("ready"):
+
+        @pl.when(at_end)
+        def _():
+            pl.semaphore_wait(ready_sem, 1)
+
+    for copy in e_copies:
+        copy.start()
 
     has_fwd_out = ((core == 0) & (lat < 14)) | ((core == 1) & (lat >= 2))
     has_fwd_in = ((core == 1) & (lat < 14)) | ((core == 0) & (lat >= 2))
@@ -172,12 +191,11 @@
         pl.when(has_relay_to)(lambda: z_copy(h, n).start())
         pl.when(core == y_lo)(lambda: f_copy(h, n).start())
 
-    def on_q(h):
+    def on_q(h, n):
         @pl.when(has_relay_from)
         def _():
-            for n in range(PIECES):
-                z_copy(h, n).wait_recv()
-                pl.when(core != y_lo)(lambda n=n: f_copy(h, n).start())
+            z_copy(h, n).wait_recv()
+            pl.when(core != y_lo)(lambda: f_copy(h, n).start())
 
     def tiles_in(h):
         for n in range(PIECES):
@@ -237,18 +255,19 @@
             b_copy(h, 1, i).start()
 
     with jax.named_scope("relay0"):
-        on_p(0, 0)
-        on_p(0, 1)
+        for n in range(PIECES):
+            on_p(0, n)
+    with jax.named_scope("edges"):
         for copy in e_copies:
             copy.wait_recv()
         rims[8:12] = edge_in[0] + edge_in[1]
         for d in NEAR:
             pl.when(inside(lat + d))(lambda d=d: m_copy(d).start())
-        send_own(1)
-        for n in range(2, PIECES):
-            on_p(0, n)
     with jax.named_scope("q0"):
-        on_q(0)
+        for n in range(PIECES):
+            on_q(0, n)
+            if n + 1 < PIECES:
+                on_p(1, n)
     with jax.named_scope("weights"):
         for copy in (*w_copies, *id_copies):
             copy.wait()
@@ -259,21 +278,19 @@
         tiles_in(0)
     stencil(0)
     outward(0, 0)
-    for h in range(1, PARTS):
-        with jax.named_scope("p1"):
-            for n in range(PIECES):
-                on_p(h, n)
-        outward(h - 1, 1)
-        outward(h - 1, 2)
-        with jax.named_scope("q1"):
-            on_q(h)
-        outward(h - 1, 3)
-        with jax.named_scope("tiles1"):
-            tiles_in(h)
-        stencil(h)
-        outward(h, 0)
-    for i in range(1, STEPS):
-        outward(PARTS - 1, i)
+    with jax.named_scope("p1"):
+        on_p(1, PIECES - 1)
+    outward(0, 1)
+    outward(0, 2)
+    with jax.named_scope("q1"):
+        for n in range(PIECES):
+            on_q(1, n)
+    outward(0, 3)
+    with jax.named_scope("tiles1"):
+        tiles_in(1)
+    stencil(1)
+    for i in range(STEPS):
+        outward(1, i)
     with jax.named_scope("inward"):
         half = TGT // 2
         x = x_ref[...]
@@ -336,7 +353,7 @@
             pltpu.VMEM((PARTS, TGT, WIDTH), BF16),
             pltpu.VMEM((PARTS, TGT, WIDTH), BF16),
             pltpu.VMEM((PARTS, TGT, WIDTH), BF16),
-            dma((PARTS,)), dma((W_COPIES,)), dma((2,)),
+            dma((PARTS,)), dma((W_COPIES,)), dma((2,)), pltpu.SemaphoreType.REGULAR,
             dma((PARTS, PIECES)), dma((PARTS, PIECES)),
             dma((PARTS, PIECES)), dma((PARTS, PIECES)),
             dma((PARTS, PIECES)), dma((PARTS, PIECES)),

time: 36.4 us -> 34.1 us (0.937)
  Pallas kernels: 34.8 us -> 32.3 us
    pallas_call x1, Pallas kernels: 34.8 us -> 32.3 us  [body(): pl.pallas_call(kernel, out_shape=jax.ShapeDtypeStruct((TGT, CHAN), BF16),...]
where the time goes in v3:
time: 34.1 us; the launch traced here: 33.7 us
  Pallas kernels  32.3 us (95%)
  local copies, waits for them, and re-layouts  0.8 us (2%)
  between operations  0.66 us (2%)
    pallas_call x1, Pallas kernels, body(): pl.pallas_call(kernel, out_shape=jax.ShapeDtypeStruct((TGT, CHAN), BF16),...  32.3 us
    unnamed x1, local copies, waits for them, and re-layouts  0.8 us

profile of v3, /device:TPU:9, one launch (start us, length us, event | category | flops | bytes accessed | tf_op | source)
XLA Modules:
  0.0 33.7 jit_solution(11734700784700761650)
XLA Ops:
  0.7 32.3 %shard_map.46 = bf16[1024,256]{1,0:T(8,128)(2,1)S(1)} custom-call(s32[1,8]{1,0:T(1,128)} %ids_hbm.1, s32[1]{0:T(128)S(6)} %copy.6.counts_hbm, bf16[16,32,256]{2,1,0:T(8,128)(2,1)} %field_ref.1, bf16[1,1,3072,3072]{3,2,1,0:T(8,128)(2,1)} %w_ref.1), custom_call_target="tpu_custom_call" | custom-call | tf_op jit(solution)/shard_map/pallas_call | solution.py:336
  32.9 0.8 %copy.7 = bf16[1024,256]{1,0:T(8,128)(2,1)} copy(bf16[1024,256]{1,0:T(8,128)(2,1)S(1)} %shard_map.46) | data formatting | bytes 1048576
